TPU v7x, 32 devices: a whole 2x2x4 slice. The times are simulated.
32 devices in a mesh: dp: 2 (over core), vocab: 16 (over z, y, x).
Axes of the slice: x: 2, y: 2, z: 4, core: 2. Of those that a mesh axis runs over, the one named last changes fastest.
Arguments:
- table: bfloat16 [16384, 4096], P('vocab'), may hold values from -0.75 to 0.75
- hidden: bfloat16 [512, 4096], P(('dp', 'vocab')), may hold values from -9 to 9
- cotangent: bfloat16 [512, 4096], P(('dp', 'vocab')), may hold values from -0.75 to 0.75
- input_ids: int32 [512], P('dp'), may hold values from 0 to 16383, as said below
- target_ids: int32 [512], P('dp'), may hold values from 0 to 16383
Outputs:
- table_grad: float32 [16384, 4096], P(('vocab', 'dp'))
- hidden_grad: bfloat16 [512, 4096], P(('dp', 'vocab'))
- token_loss: float32 [512], P('dp')
Inputs may be any that keep to these rules, and one draw needn't show every extreme that they name: `input_ids`: the ids of one replica group may all lie in the 1024 rows of one index of vocab; in every draw some group's ids do.
All inputs are finite; a program needn't handle non-finite values.
Results may differ from a plain program's by a relative error of at most 0.0034.
Values may be sent and summed in bfloat16 or wider, within the bound.
A program may use at most 128 MiB of HBM per device.

v0:
```python
import jax
import jax.numpy as jnp
from jax import lax
from jax.sharding import PartitionSpec as P


def shards(table, hidden, cotangent, input_ids, target_ids):
    shard_rows = table.shape[0]
    width = table.shape[1]
    offset = lax.axis_index("vocab") * shard_rows
    rows = lax.all_gather(hidden, "vocab", axis=0, tiled=True)
    incoming = lax.all_gather(cotangent, "vocab", axis=0, tiled=True)
    logits = lax.dot_general(
        rows, table, (((1,), (1,)), ((), ())), preferred_element_type=jnp.float32
    )
    columns = offset + jnp.arange(shard_rows, dtype=jnp.int32)
    hit = target_ids[:, None] == columns[None, :]
    local_pick = jnp.sum(jnp.where(hit, logits, jnp.float32(0.0)), axis=1)
    local_max = jnp.max(logits, axis=1)
    top = lax.pmax(local_max, "vocab")
    local_total = jnp.sum(jnp.exp(logits - top[:, None]), axis=1)
    total, picked = lax.psum((local_total, local_pick), "vocab")
    lse = top + jnp.log(total)
    token_loss = lse - picked
    dlogits = (jnp.exp(logits - lse[:, None]) - hit.astype(jnp.float32)).astype(jnp.bfloat16)
    hidden_grad = lax.psum_scatter(
        jnp.dot(dlogits, table, preferred_element_type=jnp.float32),
        "vocab",
        scatter_dimension=0,
        tiled=True,
    ).astype(jnp.bfloat16)
    local_ids = input_ids - offset
    inside = (local_ids >= 0) & (local_ids < shard_rows)
    targets = jnp.where(inside, local_ids, shard_rows)
    first_section = (
        jnp.zeros((shard_rows, width), jnp.float32)
        .at[targets]
        .add(incoming.astype(jnp.float32), mode="drop")
    )
    full = (
        lax.dot_general(dlogits, rows, (((0,), (0,)), ((), ())), preferred_element_type=jnp.float32)
        + first_section
    )
    table_grad = lax.psum_scatter(full, "dp", scatter_dimension=0, tiled=True)
    return (table_grad, hidden_grad, token_loss)


def solution(mesh):
    return jax.shard_map(
        shards,
        mesh=mesh,
        in_specs=(
            P("vocab", None),
            P(("dp", "vocab"), None),
            P(("dp", "vocab"), None),
            P("dp"),
            P("dp"),
        ),
        out_specs=(P(("vocab", "dp"), None), P(("dp", "vocab"), None), P("dp")),
        check_vma=False,
    )
```

profile of v0, /device:TPU:0, one launch (start us, length us, event | category | flops | bytes accessed | tf_op | source)
XLA Modules:
  0.0 292.8 jit_solution(14492816868424003785)
XLA Ops:
  7.2 0.0 all-gather.3.cloned.1.call-start
  7.2 0.7 all-gather.3.cloned.1.call-update
  7.9 0.0 all-gather.5.cloned.1.call-start
  7.9 0.7 all-gather.5.cloned.1.call-update
  8.6 0.0 reduce-scatter.5.cloned.1.call-start
  8.7 0.0 copy-start.1
  8.7 65.2 %all-gather.3.cloned.1.call-done = bf16[256,4096]{1,0:T(8,128)(2,1)} async-done(((bf16[16,4096]{1,0:T(8,128)(2,1)}), bf16[256,4096]{1,0:T(8,128)(2,1)}) %all-gather.3.cloned.1.call-update) | async-done | bytes 2097168 | tf_op jit(solution)/shard_map/all_gather | solution.py:11
  73.9 6.5 %fusion.10 = (f32[256]{0:T(256)S(1)}, f32[256,1024]{1,0:T(8,128)S(1)}) fusion(bf16[256,4096]{1,0:T(8,128)(2,1)} %all-gather.3.cloned.1.call-done, bf16[1024,4096]{1,0:T(8,128)(2,1)} %param.5), kind=kOutput, calls=%fused_computation.16 | convolution fusion | flops 2147745536 | bytes 11535360 | tf_op jit(solution)/shard_map/dot_general | solution.py:13
  80.3 39.8 %pmax.7 = f32[256]{0:T(256)S(1)} all-reduce(f32[256]{0:T(256)S(1)} %get-tuple-element.9), channel_id=1, replica_groups=mesh['dp'=2,'vocab'=16] {'vocab'}, use_global_device_ids=true, to_apply=%region_1.2 | all-reduce | flops 256 | bytes 2048 | tf_op jit(solution)/shard_map/pmax | solution.py:20
  120.2 0.0 copy-done.1
  120.2 0.4 fusion.4
  120.6 36.9 %all-reduce = (f32[256]{0:T(256)S(1)}, f32[256]{0:T(256)S(1)}) all-reduce(f32[256]{0:T(256)S(1)} %get-tuple-element.4, f32[256]{0:T(256)S(1)} %get-tuple-element.3), channel_id=1, replica_groups=mesh['dp'=2,'vocab'=16] {'vocab'}, use_global_device_ids=true, to_apply=%region_3.4 | all-reduce | flops 512 | bytes 4096 | tf_op jit(solution)/shard_map/psum | solution.py:22
  157.4 0.6 fusion.9
  158.0 7.8 %fusion.5 = f32[256,4096]{1,0:T(8,128)} fusion(bf16[1024,4096]{1,0:T(8,128)(2,1)} %param.5, f32[256,1024]{1,0:T(8,128)S(1)} %get-tuple-element.10, s32[1024]{0:T(1024)S(1)} %iota_add_fusion, f32[256]{0:T(256)S(1)} %get-tuple-element.8, s32[256]{0:T(256)S(1)} %copy-done.1), kind=kOutput, calls=%fused_computation.13 | convolution fusion | flops 2148794368 | bytes 13637632 | tf_op jit(solution)/shard_map/dot_general | solution.py:27
  165.8 0.0 copy-start.2
  165.8 0.0 copy-start
  165.8 0.0 reduce-scatter.5.cloned.1.call-update
  165.8 0.2 reduce-scatter.3.cloned.1.call-start
  166.1 0.4 copy-done.2
  166.5 0.9 copy-done
  167.4 8.2 %fusion.7 = f32[1024,4096]{1,0:T(8,128)} fusion(bf16[256,4096]{1,0:T(8,128)(2,1)S(1)} %copy-done, f32[256,1024]{1,0:T(8,128)S(1)} %get-tuple-element.10, s32[1024]{0:T(1024)S(1)} %iota_add_fusion, f32[256]{0:T(256)S(1)} %get-tuple-element.8, s32[256]{0:T(256)S(1)} %copy-done.1), kind=kOutput, calls=%fused_computation.14 | convolution fusion | flops 2148794368 | bytes 19929088 | tf_op jit(solution)/shard_map/dot_general | solution.py:41
  175.6 0.0 all-gather.5.cloned.1.call-done
  175.6 18.7 %scatter_custom_fusion = f32[1024,4096]{1,0:T(8,128)} fusion(f32[1024,4096]{1,0:T(8,128)} %fusion.7, s32[256]{0:T(256)S(1)} %compare_select_fusion.1, bf16[256,4096]{1,0:T(8,128)(2,1)} %all-gather.5.cloned.1.call-done), kind=kCustom, calls=%fused_computation.1 | custom fusion | flops 2097152 | bytes 18874368 | tf_op jit(solution)/shard_map/scatter-add | solution.py:38
  194.4 0.0 reduce-scatter.3.cloned.1.call-update
  194.4 64.5 %reduce-scatter.5.cloned.1.call-done = f32[16,4096]{1,0:T(8,128)} async-done(((f32[256,4096]{1,0:T(8,128)}), f32[16,4096]{1,0:T(8,128)}) %reduce-scatter.5.cloned.1.call-update) | async-done | bytes 262160 | tf_op jit(solution)/shard_map/reduce_scatter | solution.py:26
  258.9 1.6 convert_element_type.15
  260.5 25.7 %reduce-scatter.3.cloned.1.call-done = f32[512,4096]{1,0:T(8,128)} async-done(((f32[1024,4096]{1,0:T(8,128)}), f32[512,4096]{1,0:T(8,128)}) %reduce-scatter.3.cloned.1.call-update) | async-done | bytes 8388624 | tf_op jit(solution)/shard_map/reduce_scatter | solution.py:44
  (2 shorter events, 0.0 us)
Async XLA Ops:
  7.2 66.7 %all-gather.3.cloned.1.call-start = ((), (), s32[]{:S(2)}) async-start(), calls=%async_computation.2 | async-start | bytes 2228224 | tf_op jit(solution)/shard_map/all_gather | solution.py:11
  7.9 167.7 %all-gather.5.cloned.1.call-start = ((), (), s32[]{:S(2)}) async-start(), calls=%async_computation.3 | async-start | bytes 2228224 | tf_op jit(solution)/shard_map/all_gather | solution.py:12
  8.6 250.2 %reduce-scatter.5.cloned.1.call-start = ((), (), s32[]{:S(2)}) async-start(), calls=%async_computation.5 | async-start | bytes 4456448 | tf_op jit(solution)/shard_map/reduce_scatter | solution.py:26
  8.7 111.4 %copy-start.1 = (s32[256]{0:T(256)S(1)}, s32[256]{0:T(256)}, u32[]{:S(2)}) copy-start(s32[256]{0:T(256)} %param.9) | copy-start | bytes 3076
  165.8 0.7 copy-start.2
  165.8 1.6 copy-start
  165.8 120.4 %reduce-scatter.3.cloned.1.call-start = ((), (), s32[]{:S(2)}) async-start(), calls=%async_computation.4 | async-start | bytes 25165824 | tf_op jit(solution)/shard_map/reduce_scatter | solution.py:44
Sparse Core Ops, SparseCore 0:
  10.7 63.0 all-gather.2
  76.6 59.4 all-gather.4
  165.9 92.8 reduce-scatter.4
  261.6 24.5 reduce-scatter.2
where the time goes:
time: 293 us
  waiting for transfers between devices  157 us (54%)
  blocking collectives  76.7 us (26%)
  matrix products  22.5 us (8%)
  other arithmetic  21.3 us (7%)
  between operations  13.8 us (5%)
    all_gather x1, waiting for transfers between devices, shards(): rows = lax.all_gather(hidden, 'vocab', axis=0, tiled=True)  65.2 us
    reduce_scatter x1, waiting for transfers between devices, shards(): lax.psum_scatter(jnp.dot(dlogits, table, preferred_element_type=jnp.float...  64.5 us
    pmax x1, blocking collectives, shards(): top = lax.pmax(local_max, 'vocab')  39.8 us
    psum x1, blocking collectives, shards(): total, picked = lax.psum((local_total, local_pick), 'vocab')  36.9 us
    reduce_scatter x1, waiting for transfers between devices, shards(): table_grad = lax.psum_scatter(full, 'dp', scatter_dimension=0, tiled=True)  25.7 us
    scatter-add x1, other arithmetic, shards(): first_section = jnp.zeros((shard_rows, width), jnp.float32).at[targets].a...  18.7 us
    dot_general x1, matrix products, shards(): lax.dot_general(dlogits, rows, (((0,), (0,)), ((), ())), preferred_elemen...  8.23 us
    dot_general x1, matrix products, shards(): jnp.dot(dlogits, table, preferred_element_type=jnp.float32)  7.77 us
  transfers between devices with their start and end apart: 4, of which 3 were waited for; matrix products, arithmetic and copies ran while one was open for 15% of the time, Pallas kernels for 0%

commit v1 on v0

--- a/solution.py
+++ b/solution.py
@@ -8,8 +8,13 @@
     shard_rows = table.shape[0]
     width = table.shape[1]
     offset = lax.axis_index("vocab") * shard_rows
-    rows = lax.all_gather(hidden, "vocab", axis=0, tiled=True)
-    incoming = lax.all_gather(cotangent, "vocab", axis=0, tiled=True)
+    rows, incoming = jnp.split(
+        jax.lax.all_gather(
+            jnp.concatenate([hidden, cotangent], axis=1), "vocab", axis=0, tiled=True
+        ),
+        [hidden.shape[1]],
+        axis=1,
+    )
     logits = lax.dot_general(
         rows, table, (((1,), (1,)), ((), ())), preferred_element_type=jnp.float32
     )

time: 293 us -> 308 us (1.051)
  waiting for transfers between devices: 157 us -> 171 us
    all_gather x2 -> x1, waiting for transfers between devices: 65.2 us -> 80.7 us  [shards(): jax.lax.all_gather(jnp.concatenate([hidden, cotangent], axis=1), 'vocab',...]
  transfers between devices with their start and end apart: 4 -> 3, of which waited for: 3 -> 3; matrix products, arithmetic and copies ran while one was open for 15% -> 10% of each run, Pallas kernels for 0% -> 0%
where the time goes in v1:
time: 308 us
  waiting for transfers between devices  171 us (56%)
  blocking collectives  75.9 us (25%)
  matrix products  24.1 us (8%)
  other arithmetic  23 us (7%)
  between operations  13.8 us (4%)
    all_gather x1, waiting for transfers between devices, shards(): jax.lax.all_gather(jnp.concatenate([hidden, cotangent], axis=1), 'vocab',...  80.7 us
    reduce_scatter x1, waiting for transfers between devices, shards(): lax.psum_scatter(jnp.dot(dlogits, table, preferred_element_type=jnp.float...  64 us
    pmax x1, blocking collectives, shards(): top = lax.pmax(local_max, 'vocab')  39.4 us
    psum x1, blocking collectives, shards(): total, picked = lax.psum((local_total, local_pick), 'vocab')  36.6 us
    reduce_scatter x1, waiting for transfers between devices, shards(): table_grad = lax.psum_scatter(full, 'dp', scatter_dimension=0, tiled=True)  25.9 us
    scatter-add x1, other arithmetic, shards(): first_section = jnp.zeros((shard_rows, width), jnp.float32).at[targets].a...  18.7 us
    dot_general x1, matrix products, shards(): lax.dot_general(dlogits, rows, (((0,), (0,)), ((), ())), preferred_elemen...  9.82 us
    dot_general x1, matrix products, shards(): jnp.dot(dlogits, table, preferred_element_type=jnp.float32)  7.78 us
  transfers between devices with their start and end apart: 3, of which 3 were waited for; matrix products, arithmetic and copies ran while one was open for 10% of the time, Pallas kernels for 0%

profile of v1, /device:TPU:0, one launch (start us, length us, event | category | flops | bytes accessed | tf_op | source)
XLA Modules:
  0.0 308.1 jit_solution(10558892179661774579)
XLA Ops:
  7.2 0.0 all-gather.2.cloned.1.call-start
  7.2 1.7 pad_maximum_fusion
  8.9 0.0 all-gather.2.cloned.1.call-update
  8.9 0.0 reduce-scatter.5.cloned.1.call-start
  9.0 0.0 copy-start
  9.0 80.7 %all-gather.2.cloned.1.call-done = bf16[256,8192]{1,0:T(8,128)(2,1)} async-done(((bf16[16,8192]{1,0:T(8,128)(2,1)}), bf16[256,8192]{1,0:T(8,128)(2,1)}) %all-gather.2.cloned.1.call-update) | async-done | bytes 4194320 | tf_op jit(solution)/shard_map/all_gather | solution.py:12
  89.7 6.5 %fusion.14 = (f32[256]{0:T(256)S(1)}, f32[256,1024]{1,0:T(8,128)S(1)}) fusion(bf16[1024,4096]{1,0:T(8,128)(2,1)} %param.5, bf16[256,8192]{1,0:T(8,128)(2,1)} %all-gather.2.cloned.1.call-done), kind=kOutput, calls=%fused_computation.21 | convolution fusion | flops 2147745536 | bytes 11535360 | tf_op jit(solution)/shard_map/dot_general | solution.py:18
  96.1 39.4 %pmax.7 = f32[256]{0:T(256)S(1)} all-reduce(f32[256]{0:T(256)S(1)} %get-tuple-element.9), channel_id=1, replica_groups=mesh['dp'=2,'vocab'=16] {'vocab'}, use_global_device_ids=true, to_apply=%region_1.2 | all-reduce | flops 256 | bytes 2048 | tf_op jit(solution)/shard_map/pmax | solution.py:25
  135.5 0.0 copy-done
  135.5 0.4 fusion.9
  135.9 36.6 %all-reduce = (f32[256]{0:T(256)S(1)}, f32[256]{0:T(256)S(1)}) all-reduce(f32[256]{0:T(256)S(1)} %get-tuple-element.4, f32[256]{0:T(256)S(1)} %get-tuple-element.3), channel_id=1, replica_groups=mesh['dp'=2,'vocab'=16] {'vocab'}, use_global_device_ids=true, to_apply=%region_3.4 | all-reduce | flops 512 | bytes 4096 | tf_op jit(solution)/shard_map/psum | solution.py:27
  172.5 0.6 fusion.13
  173.0 7.8 %fusion.10 = f32[256,4096]{1,0:T(8,128)} fusion(bf16[1024,4096]{1,0:T(8,128)(2,1)} %param.5, f32[256,1024]{1,0:T(8,128)S(1)} %get-tuple-element.10, s32[1024]{0:T(1024)S(1)} %iota_add_fusion, f32[256]{0:T(256)S(1)} %get-tuple-element.8, s32[256]{0:T(256)S(1)} %copy-done), kind=kOutput, calls=%fused_computation.19 | convolution fusion | flops 2148794368 | bytes 13637632 | tf_op jit(solution)/shard_map/dot_general | solution.py:32
  180.8 0.0 copy-start.1
  180.8 0.0 reduce-scatter.5.cloned.1.call-update
  180.9 0.2 reduce-scatter.3.cloned.1.call-start
  181.1 0.4 copy-done.1
  181.5 9.8 %fusion.3 = f32[1024,4096]{1,0:T(8,128)} fusion(bf16[256,8192]{1,0:T(8,128)(2,1)} %all-gather.2.cloned.1.call-done, f32[256,1024]{1,0:T(8,128)S(1)} %get-tuple-element.10, s32[1024]{0:T(1024)S(1)} %iota_add_fusion, f32[256]{0:T(256)S(1)} %get-tuple-element.8, s32[256]{0:T(256)S(1)} %copy-done), kind=kOutput, calls=%fused_computation.4 | convolution fusion | flops 2148794368 | bytes 19929088 | tf_op jit(solution)/shard_map/dot_general | solution.py:46
  191.3 18.7 %scatter_custom_fusion = f32[1024,4096]{1,0:T(8,128)} fusion(f32[1024,4096]{1,0:T(8,128)} %fusion.3, s32[256]{0:T(256)S(1)} %compare_select_fusion.1, bf16[256,8192]{1,0:T(8,128)(2,1)} %all-gather.2.cloned.1.call-done), kind=kCustom, calls=%fused_computation.1 | custom fusion | flops 2097152 | bytes 18874368 | tf_op jit(solution)/shard_map/scatter-add | solution.py:43
  210.1 0.0 reduce-scatter.3.cloned.1.call-update
  210.1 64.0 %reduce-scatter.5.cloned.1.call-done = f32[16,4096]{1,0:T(8,128)} async-done(((f32[256,4096]{1,0:T(8,128)}), f32[16,4096]{1,0:T(8,128)}) %reduce-scatter.5.cloned.1.call-update) | async-done | bytes 262160 | tf_op jit(solution)/shard_map/reduce_scatter | solution.py:31
  274.1 1.6 convert_element_type.15
  275.7 25.9 %reduce-scatter.3.cloned.1.call-done = f32[512,4096]{1,0:T(8,128)} async-done(((f32[1024,4096]{1,0:T(8,128)}), f32[512,4096]{1,0:T(8,128)}) %reduce-scatter.3.cloned.1.call-update) | async-done | bytes 8388624 | tf_op jit(solution)/shard_map/reduce_scatter | solution.py:49
  (2 shorter events, 0.0 us)
Async XLA Ops:
  7.2 82.5 %all-gather.2.cloned.1.call-start = ((), (), s32[]{:S(2)}) async-start(), calls=%async_computation.2 | async-start | bytes 4456448 | tf_op jit(solution)/shard_map/all_gather | solution.py:12
  8.9 265.2 %reduce-scatter.5.cloned.1.call-start = ((), (), s32[]{:S(2)}) async-start(), calls=%async_computation.4 | async-start | bytes 4456448 | tf_op jit(solution)/shard_map/reduce_scatter | solution.py:31
  9.0 126.5 %copy-start = (s32[256]{0:T(256)S(1)}, s32[256]{0:T(256)}, u32[]{:S(2)}) copy-start(s32[256]{0:T(256)} %param.9) | copy-start | bytes 3076
  180.8 0.7 copy-start.1
  180.9 120.7 %reduce-scatter.3.cloned.1.call-start = ((), (), s32[]{:S(2)}) async-start(), calls=%async_computation.3 | async-start | bytes 25165824 | tf_op jit(solution)/shard_map/reduce_scatter | solution.py:49
Sparse Core Ops, SparseCore 0:
  11.3 78.3 all-gather.1
  181.0 93.0 reduce-scatter.4
  277.0 24.5 reduce-scatter.2
